TPU v7x, 32 devices: a whole 2x2x4 slice. The times are simulated.
32 devices in a mesh: dp: 4 (over y, x), fsdp: 8 (over z, core).
Axes of the slice: x: 2, y: 2, z: 4, core: 2. Of those that a mesh axis runs over, the one named last changes fastest.
Arguments:
- grads: bfloat16 [4, 16, 512, 512], P('dp', None, 'fsdp'), may hold values from -4 to 4
- left_stats: float32 [8, 4, 512, 512], P('fsdp', None, 'dp'), may hold values from -0.5 to 9, as said below
- right_stats: float32 [8, 4, 512, 512], P('fsdp', None, 'dp'), may hold values from -0.5 to 9, as said below
- left_root: bfloat16 [8, 4, 512, 512], P('fsdp', None, 'dp'), may hold values from -0.5 to 14, as said below
- right_root: bfloat16 [8, 4, 512, 512], P('fsdp'), may hold values from -0.5 to 14, as said below
- second_moment: float32 [8, 4, 512, 512], P('fsdp', None, 'dp'), may hold values from 0.2 to 2
- slot_block: int32 [8, 4], replicated, may hold values from 0 to 15, as said below
- counts: int32 [8], replicated, may hold values from 0 to 4, as said below
Outputs:
- left_new: float32 [8, 4, 512, 512], P('fsdp', None, 'dp')
- right_new: float32 [8, 4, 512, 512], P('fsdp', None, 'dp')
- second_new: float32 [8, 4, 512, 512], P('fsdp', None, 'dp')
- update: float32 [8, 4, 512, 512], P('fsdp', None, 'dp')
Inputs may be any that keep to these rules, and one draw needn't show every extreme that they name: Every owner holds counts[o] blocks; the counts sum to 16, and some owner holds exactly 4. `slot_block`: the first counts[o] slots of owner o name distinct blocks, every block is named by exactly one such slot, and later slots name arbitrary blocks. `left_stats`: Symmetric. `right_stats`: Symmetric. `left_root`: Symmetric. `right_root`: Symmetric.
All inputs are finite; a program needn't handle non-finite values.
Results may differ from a plain program's by a relative error of at most 0.015.
Values may be sent and summed in bfloat16 or wider, within the bound.
No kernel may reach another device: no remote copies, remote signals or barrier semaphores. Data moves between devices by JAX's collectives and lax.ppermute only.
A program may use at most 64 MiB of HBM per device.

v0:
```python
import jax
import jax.numpy as jnp
from jax import lax
from jax.sharding import PartitionSpec as P

SHAMPOO_BETA = 0.998
ADAM_BETA = 0.95
EPSILON = 1e-08


def on_device(
    grads, left_stats, right_stats, left_root, right_root, second_moment, slot_block, counts
):
    slot_count = slot_block.shape[1]
    owner_count = slot_block.shape[0]
    block_order = left_root.shape[3]
    partial_value = grads[0]
    block_count = partial_value.shape[0]
    slab_rows = partial_value.shape[1]
    flat_slots = slot_block.reshape(-1)
    live_slots = (jnp.arange(slot_count, dtype=jnp.int32)[None, :] < counts[:, None]).reshape(-1)
    flat_partial = partial_value.reshape(block_count, slab_rows * block_order).astype(jnp.float32)
    summed = lax.psum_scatter(
        flat_partial.astype(jnp.bfloat16), "dp", scatter_dimension=1, tiled=True
    )
    picked = jnp.where(live_slots[:, None], summed[flat_slots], jnp.zeros((), jnp.bfloat16))
    received = lax.all_to_all(picked, "fsdp", split_axis=0, concat_axis=1, tiled=True)
    piece_width = summed.shape[1]
    received = received.reshape(slot_count, owner_count, piece_width)
    gathered = lax.all_gather(received, "dp", axis=2, tiled=True)
    grad_full = gathered.reshape(slot_count, block_order, block_order)
    slab_width = block_order // lax.axis_size("dp")
    row_start = lax.axis_index("dp") * slab_width
    row_grad = lax.dynamic_slice_in_dim(grad_full, row_start, slab_width, 1)
    column_grad = lax.dynamic_slice_in_dim(grad_full, row_start, slab_width, 2)
    owned_here = jnp.arange(slot_count, dtype=jnp.int32) < counts[lax.axis_index("fsdp")]
    keep_mask = owned_here[:, None, None]
    left_term = jnp.einsum("crk,cjk->crj", row_grad, grad_full, preferred_element_type=jnp.float32)
    right_term = jnp.einsum(
        "ckr,ckj->crj", column_grad, grad_full, preferred_element_type=jnp.float32
    )
    left_old = left_stats[0]
    right_old = right_stats[0]
    left_new = jnp.where(
        keep_mask, SHAMPOO_BETA * left_old + (1.0 - SHAMPOO_BETA) * left_term, left_old
    )
    right_new = jnp.where(
        keep_mask, SHAMPOO_BETA * right_old + (1.0 - SHAMPOO_BETA) * right_term, right_old
    )
    left_half = jnp.einsum(
        "crk,ckj->crj", left_root[0], grad_full, preferred_element_type=jnp.float32
    ).astype(jnp.bfloat16)
    precond = jnp.einsum(
        "crk,ckj->crj", left_half, right_root[0], preferred_element_type=jnp.float32
    )
    row_values = row_grad.astype(jnp.float32)
    moment_old = second_moment[0]
    second_new = jnp.where(
        keep_mask, ADAM_BETA * moment_old + (1.0 - ADAM_BETA) * row_values * row_values, moment_old
    )
    adam = row_values / (jnp.sqrt(second_new) + EPSILON)
    precond_sum, adam_sum = lax.psum(
        (jnp.sum(precond * precond, axis=(1, 2)), jnp.sum(adam * adam, axis=(1, 2))), "dp"
    )
    graft_scale = jnp.where(
        owned_here, jnp.sqrt(adam_sum / jnp.where(owned_here, precond_sum, 1.0)), 0.0
    )
    update = precond * graft_scale[:, None, None]
    return (left_new[None], right_new[None], second_new[None], update[None])


def solution(mesh):
    in_specs = (
        P("dp", None, "fsdp", None),
        P("fsdp", None, "dp", None),
        P("fsdp", None, "dp", None),
        P("fsdp", None, "dp", None),
        P("fsdp", None, None, None),
        P("fsdp", None, "dp", None),
        P(),
        P(),
    )
    out_specs = (
        P("fsdp", None, "dp", None),
        P("fsdp", None, "dp", None),
        P("fsdp", None, "dp", None),
        P("fsdp", None, "dp", None),
    )
    return jax.shard_map(
        on_device, mesh=mesh, in_specs=in_specs, out_specs=out_specs, check_vma=False
    )
```

profile of v0, /device:TPU:0, one launch (start us, length us, event | category | flops | bytes accessed | tf_op | source)
XLA Modules:
  0.0 133.5 jit_solution(11357918869581016705)
XLA Ops:
  7.2 0.0 copy-start
  7.2 0.0 copy-start.4
  7.2 0.0 copy-start.5
  7.2 0.0 reduce-scatter.2.cloned.1.call-start
  7.2 2.9 %copy.26 = bf16[2,8,64,512]{3,1,2,0:T(8,128)(2,1)} copy(bf16[2,8,64,512]{3,2,1,0:T(8,128)(2,1)} %bitcast.50) | data formatting | bytes 2097152
  10.2 0.0 reduce-scatter.2.cloned.1.call-update
  10.2 0.0 all-gather.2.cloned.1.call-start
  10.2 0.0 copy-done.4
  10.2 0.1 copy.18
  10.3 0.1 reshape.70
  10.4 0.0 copy-done.5
  10.4 0.1 iota_compare_fusion
  10.5 31.7 %reduce-scatter.2.cloned.1.call-done = bf16[16,8192]{1,0:T(8,128)(2,1)} async-done(((bf16[16,32768]{1,0:T(8,128)(2,1)}), bf16[16,8192]{1,0:T(8,128)(2,1)}) %reduce-scatter.2.cloned.1.call-update) | async-done | bytes 262160 | tf_op jit(solution)/shard_map/reduce_scatter | solution.py:23
  42.2 2.3 %gather_fusion = bf16[32,8192]{1,0:T(8,128)(2,1)S(1)} fusion(bf16[16,8192]{1,0:T(8,128)(2,1)} %reduce-scatter.2.cloned.1.call-done, s32[1024]{0:T(1024)S(1)} %pad_clamp_fusion), kind=kCustom, calls=%fused_computation | custom fusion | bytes 1048704 | tf_op jit(solution)/shard_map/gather | solution.py:26
  44.5 0.2 gather.6
  44.7 0.3 broadcast_select_fusion
  45.0 19.8 %all_to_all.13 = bf16[8,4,8192]{2,1,0:T(4,128)(2,1)} all-to-all(bf16[8,4,8192]{2,1,0:T(4,128)(2,1)S(1)} %broadcast_select_fusion), channel_id=1, replica_groups=mesh['dp'=4,'fsdp'=8] {'fsdp'}, dimensions={0} | all-to-all | bytes 1048576 | tf_op jit(solution)/shard_map/all_to_all | solution.py:27
  64.8 0.0 all-gather.2.cloned.1.call-update
  64.9 0.6 dynamic_slice.9
  65.4 0.6 iota_compare_fusion.1
  66.1 32.0 %all-gather.2.cloned.1.call-done = bf16[4,8,32768]{2,0,1:T(4,128)(2,1)} async-done(((bf16[4,8,8192]{2,0,1:T(4,128)(2,1)}), bf16[4,8,32768]{2,0,1:T(4,128)(2,1)}) %all-gather.2.cloned.1.call-update) | async-done | bytes 2097168 | tf_op jit(solution)/shard_map/all_gather | solution.py:30
  98.1 4.1 %copy.19 = bf16[4,8,32768]{2,1,0:T(8,128)(2,1)} copy(bf16[4,8,32768]{2,0,1:T(4,128)(2,1)} %all-gather.2.cloned.1.call-done) | data formatting | bytes 4194304 | tf_op jit(solution)/shard_map/all_gather | solution.py:30
  102.2 4.3 %reshape.71 = bf16[4,512,512]{2,1,0:T(8,128)(2,1)} reshape(bf16[4,8,32768]{2,1,0:T(8,128)(2,1)} %copy.19) | data formatting | bytes 4194304 | tf_op jit(solution)/shard_map/reshape | solution.py:31
  106.5 3.1 %fusion.11 = (f32[4]{0:T(128)S(1)}, f32[1,4,128,512]{3,2,1,0:T(8,128)}) fusion(f32[1,4,128,512]{3,2,1,0:T(8,128)} %param.13, pred[4]{0:T(512)(128)(4,1)S(1)} %iota_compare_fusion.1, bf16[4,512,512]{2,1,0:T(8,128)(2,1)} %reshape.71, s32[]{:T(128)S(6)} %select_n.42), kind=kLoop, calls=%fused_computation.22 | loop fusion | flops 2621436 | bytes 2621464 | tf_op jit(solution)/shard_map/reduce_sum | solution.py:63
  109.6 0.0 copy-done.2
  109.6 0.0 copy-done.1
  109.6 1.5 %fusion.4 = f32[1,4,128,512]{3,2,1,0:T(8,128)} fusion(bf16[4,512,512]{2,1,0:T(8,128)(2,1)S(1)} %copy-done.1, f32[1,4,128,512]{3,2,1,0:T(8,128)S(1)} %copy-done.2, s32[]{:T(128)S(6)} %select_n.42, pred[4]{0:T(512)(128)(4,1)S(1)} %iota_compare_fusion.1), kind=kOutput, calls=%fused_computation.7 | convolution fusion | flops 269484032 | bytes 4719108 | tf_op jit(solution)/shard_map/ckr,ckj->crj/dot_general | solution.py:39
  111.1 1.8 %fusion.7 = f32[1,4,128,512]{3,2,1,0:T(8,128)} fusion(bf16[4,512,512]{2,1,0:T(8,128)(2,1)S(1)} %copy-done.1, f32[1,4,128,512]{3,2,1,0:T(8,128)S(1)} %copy-done.3, pred[4]{0:T(512)(128)(4,1)S(1)} %iota_compare_fusion.1, s32[]{:T(128)S(6)} %select_n.42), kind=kOutput, calls=%fused_computation.11 | convolution fusion | flops 269484032 | bytes 4719108 | tf_op jit(solution)/shard_map/crk,cjk->crj/dot_general | solution.py:38
  112.9 2.9 %multiply_reduce_fusion = (f32[4]{0:T(128)S(1)}, f32[4,128,512]{2,1,0:T(8,128)S(1)}) fusion(bf16[1,4,512,512]{3,2,1,0:T(8,128)(2,1)S(1)} %copy-done, bf16[4,512,512]{2,1,0:T(8,128)(2,1)} %reshape.71, bf16[1,4,128,512]{3,2,1,0:T(8,128)(2,1)} %param.11), kind=kOutput, calls=%fused_computation.21 | convolution fusion | flops 537657344 | bytes 5767184 | tf_op jit(solution)/shard_map/crk,ckj->crj/dot_general | solution.py:53
  115.8 8.9 %all-reduce = (f32[4]{0:T(128)S(1)}, f32[4]{0:T(128)S(1)}) all-reduce(f32[4]{0:T(128)S(1)} %get-tuple-element.6, f32[4]{0:T(128)S(1)} %get-tuple-element.8), channel_id=1, replica_groups=mesh['dp'=4,'fsdp'=8] {'dp'}, use_global_device_ids=true, to_apply=%region_2.3 | all-reduce | flops 8 | bytes 64 | tf_op jit(solution)/shard_map/psum | solution.py:62
  124.8 0.7 sqrt_select_fusion
  125.4 1.2 multiply_bitcast_fusion
  (7 shorter events, 0.0 us)
Async XLA Ops:
  7.2 105.7 %copy-start = (bf16[1,4,512,512]{3,2,1,0:T(8,128)(2,1)S(1)}, bf16[1,4,512,512]{3,2,1,0:T(8,128)(2,1)}, u32[]{:S(2)}) copy-start(bf16[1,4,512,512]{3,2,1,0:T(8,128)(2,1)} %param.12) | copy-start | bytes 6291460
  7.2 3.1 %copy-start.4 = (s32[8,4]{0,1:T(4,128)S(1)}, s32[8,4]{0,1:T(4,128)}, u32[]{:S(2)}) copy-start(s32[8,4]{0,1:T(4,128)} %param.14) | copy-start | bytes 388
  7.2 3.2 %copy-start.5 = (s32[8]{0:T(128)S(1)}, s32[8]{0:T(128)}, u32[]{:S(2)}) copy-start(s32[8]{0:T(128)} %param.15) | copy-start | bytes 100
  7.2 35.0 %reduce-scatter.2.cloned.1.call-start = ((), (), s32[]{:S(2)}) async-start(), calls=%async_computation.2 | async-start | bytes 1310720 | tf_op jit(solution)/shard_map/reduce_scatter | solution.py:23
  10.2 88.0 %all-gather.2.cloned.1.call-start = ((), (), s32[]{:S(2)}) async-start(), calls=%async_computation.3 | async-start | bytes 2621440 | tf_op jit(solution)/shard_map/all_gather | solution.py:30
  102.2 7.4 %copy-start.2 = (f32[1,4,128,512]{3,2,1,0:T(8,128)S(1)}, f32[1,4,128,512]{3,2,1,0:T(8,128)}, u32[]{:S(2)}) copy-start(f32[1,4,128,512]{3,2,1,0:T(8,128)} %param.10) | copy-start | bytes 3145732
  106.5 3.1 %copy-start.1 = (bf16[4,512,512]{2,1,0:T(8,128)(2,1)S(1)}, bf16[4,512,512]{2,1,0:T(8,128)(2,1)}, u32[]{:S(2)}) copy-start(bf16[4,512,512]{2,1,0:T(8,128)(2,1)} %reshape.71) | copy-start | bytes 6291460
  109.6 1.5 %copy-start.3 = (f32[1,4,128,512]{3,2,1,0:T(8,128)S(1)}, f32[1,4,128,512]{3,2,1,0:T(8,128)}, u32[]{:S(2)}) copy-start(f32[1,4,128,512]{3,2,1,0:T(8,128)} %param.9) | copy-start | bytes 3145732
Sparse Core Ops, SparseCore 0:
  11.5 30.6 reduce-scatter.1
  65.0 33.1 all-gather.1
where the time goes:
time: 134 us; the launch traced here: 133 us
  waiting for transfers between devices  63.7 us (48%)
  blocking collectives  28.7 us (21%)
  local copies, waits for them, and re-layouts  14.5 us (11%)
  between operations  14.1 us (11%)
  matrix products  6.24 us (5%)
  other arithmetic  5.99 us (4%)
    all_gather x1, waiting for transfers between devices, on_device(): gathered = lax.all_gather(received, 'dp', axis=2, tiled=True)  32 us
    reduce_scatter x1, waiting for transfers between devices, on_device(): lax.psum_scatter(flat_partial.astype(jnp.bfloat16), 'dp', scatter_dimensi...  31.7 us
    all_to_all x1, blocking collectives, on_device(): lax.all_to_all(picked, 'fsdp', split_axis=0, concat_axis=1, tiled=True)  19.8 us
    psum x1, blocking collectives, on_device(): lax.psum((jnp.sum(precond * precond, axis=(1, 2)), jnp.sum(adam * adam, a...  8.93 us
    reshape x1, local copies, waits for them, and re-layouts, on_device(): grad_full = gathered.reshape(slot_count, block_order, block_order)  4.26 us
    all_gather x1, local copies, waits for them, and re-layouts, on_device(): gathered = lax.all_gather(received, 'dp', axis=2, tiled=True)  4.05 us
    reduce_sum x1, other arithmetic, on_device(): jnp.sum(adam * adam, axis=(1, 2))  3.12 us
    unnamed x14, local copies, waits for them, and re-layouts  3.02 us
  transfers between devices with their start and end apart: 2, of which 2 were waited for; matrix products, arithmetic and copies ran while one was open for 1% of the time, Pallas kernels for 0%

commit v1 on v0

--- a/solution.py
+++ b/solution.py
@@ -1,11 +1,422 @@
+import functools
+
 import jax
 import jax.numpy as jnp
 from jax import lax
+from jax.experimental import pallas as pl
+from jax.experimental.pallas import tpu as pltpu
 from jax.sharding import PartitionSpec as P
+
 
 SHAMPOO_BETA = 0.998
 ADAM_BETA = 0.95
 EPSILON = 1e-08
+SMALL = 8 * 1024 * 1024
+SMEM = pltpu.SMEM
+VMEM = pltpu.VMEM
+
+
+def exchange(value, axis, distance):
+    size = lax.axis_size(axis)
+    return lax.ppermute(value, axis, [(i, i ^ distance) for i in range(size)])
+
+
+def in_hbm(value):
+    return pltpu.with_memory_space_constraint(value, pltpu.HBM)
+
+
+def in_vmem(value):
+    return pltpu.with_memory_space_constraint(value, pltpu.VMEM)
+
+
+def call(kernel, out, ins, in_specs, out_specs, scratch=(), **more):
+    return pl.pallas_call(
+        kernel,
+        out_shape=out,
+        in_specs=in_specs,
+        out_specs=out_specs,
+        scratch_shapes=list(scratch),
+        compiler_params=pltpu.CompilerParams(vmem_limit_bytes=SMALL),
+        cost_estimate=pl.CostEstimate(flops=10_000_000, bytes_accessed=1_000_000, transcendentals=0),
+        **more,
+    )(*ins)
+
+
+IN_SMEM = pl.BlockSpec(memory_space=SMEM)
+IN_VMEM = pl.BlockSpec(memory_space=VMEM)
+IN_HBM = pl.BlockSpec(memory_space=pltpu.HBM)
+
+
+def slot_index(counts, meta, ways):
+    me, owner_here, owners = lax.axis_index("dp"), lax.axis_index("fsdp"), counts.shape[0]
+    start = jnp.int32(0)
+    for owner in range(owners):
+        start = start + jnp.where(owner < owner_here, counts[owner], 0)
+    for distance in range(ways):
+        meta[distance] = ((me ^ distance) - start + owners * ways * 2) % ways
+    meta[ways] = counts[owner_here]
+
+
+def deal_kernel(part, chunks, slot_block, counts, grads, *rest):
+    outs, (order, sems) = rest[:-2], rest[-2:]
+    ways, group = len(outs), outs[0].shape[0]
+    cap, owners = slot_block.shape
+    me = lax.axis_index("dp")
+    place = jnp.int32(0)
+    for owner in range(owners):
+        for slot in range(cap):
+
+            @pl.when(slot < counts[owner])
+            def _():
+                order[place + slot] = slot_block[slot, owner]
+
+        place = place + counts[owner]
+    rows = grads.shape[1] // chunks
+    copies = []
+    for distance in list(range(1, ways)) + [0]:
+        for at in range(group):
+            block = order[at * ways + (me ^ distance)]
+            sem = sems.at[distance * group + at]
+            copy = pltpu.make_async_copy(grads.at[block, pl.ds(part * rows, rows)], outs[distance].at[at], sem)
+            copy.start()
+            copies.append(copy)
+    for copy in copies:
+        copy.wait()
+
+
+def deal(slot_block, counts, grads, ways, part, chunks):
+    blocks, rows, width = grads.shape
+    return call(
+        functools.partial(deal_kernel, part, chunks),
+        (pltpu.VMEM((blocks // ways, rows // chunks, width), grads.dtype),) * ways,
+        (in_hbm(slot_block.T), in_hbm(counts), in_hbm(grads)),
+        [IN_SMEM, IN_SMEM, IN_HBM],
+        (IN_VMEM,) * ways,
+        [SMEM((blocks,), jnp.int32), pltpu.SemaphoreType.DMA((blocks,))],
+    )
+
+
+def ready_kernel(ways, counts, root, moment, meta, lent, wide, sems):
+    slot_index(counts, meta, ways)
+    slot = meta[ways - 1]
+    near = pltpu.make_async_copy(root.at[slot], lent.at[0], sems.at[0])
+    far = pltpu.make_async_copy(moment.at[slot], wide, sems.at[1])
+    near.start()
+    far.start()
+    far.wait()
+    lent[1] = wide[...].astype(lent.dtype)
+    near.wait()
+
+
+def ready(counts, root, moment, ways):
+    _, high, wide = root.shape
+    return call(
+        functools.partial(ready_kernel, ways),
+        (jax.ShapeDtypeStruct((ways + 1,), jnp.int32), pltpu.VMEM((2, high, wide), jnp.bfloat16)),
+        (in_hbm(counts), in_hbm(root), in_hbm(moment)),
+        [IN_SMEM, IN_HBM, IN_HBM],
+        (IN_SMEM, IN_VMEM),
+        [VMEM((high, wide), jnp.float32), pltpu.SemaphoreType.DMA((2,))],
+    )
+
+
+def fetch_kernel(*refs):
+    count = len(refs) // 2
+    sources, outs, sems = refs[:count], refs[count:-1], refs[-1]
+    copies = [pltpu.make_async_copy(a, b, sems.at[at]) for at, (a, b) in enumerate(zip(sources, outs))]
+    for copy in copies:
+        copy.start()
+    for copy in copies:
+        copy.wait()
+
+
+def fetch(arrays):
+    return call(
+        fetch_kernel,
+        tuple(pltpu.VMEM(x.shape, x.dtype) for x in arrays),
+        [in_hbm(x) for x in arrays],
+        [IN_HBM] * len(arrays),
+        (IN_VMEM,) * len(arrays),
+        [pltpu.SemaphoreType.DMA((len(arrays),))],
+    )
+
+
+def add_parts(parts, held):
+    total = parts[0][...].astype(jnp.float32)
+    for part in parts[1:]:
+        total = total + part[...].astype(jnp.float32)
+    held[...] = total.astype(held.dtype)
+
+
+def piece_of(counts, owner, ways):
+    start = jnp.int32(0)
+    for at in range(counts.shape[0]):
+        start = start + jnp.where(at < owner, counts[at], 0)
+    slot = (lax.axis_index("dp") - start + counts.shape[0] * ways * 2) % ways
+    return jnp.where(slot < counts[owner], (start + slot) // ways, 0)
+
+
+def sort_kernel(counts, *rest):
+    parts, (same, other, held) = rest[:-3], rest[-3:]
+    add_parts(parts, held)
+    owner_here = lax.axis_index("fsdp")
+    for distance in range(same.shape[0]):
+        same[distance] = held[piece_of(counts, owner_here ^ (2 * distance), len(parts))]
+        other[distance] = held[piece_of(counts, owner_here ^ (2 * distance + 1), len(parts))]
+
+
+def sort(counts, parts, owners):
+    group = parts[0].shape
+    half = pltpu.VMEM((owners // 2,) + group[1:], parts[0].dtype)
+    return call(
+        sort_kernel,
+        (half, half),
+        (in_hbm(counts), *[in_vmem(x) for x in parts]),
+        [IN_SMEM] + [IN_VMEM] * len(parts),
+        (IN_VMEM, IN_VMEM),
+        [VMEM(group, parts[0].dtype)],
+    )
+
+
+def pair_kernel(same, other, *outs):
+    for at, out in enumerate(outs):
+        out[0] = same[at + 1]
+        out[1] = other[at + 1]
+
+
+def pair(same, other):
+    out = pltpu.VMEM((2,) + same.shape[1:], same.dtype)
+    count = same.shape[0] - 1
+    return call(pair_kernel, (out,) * count, (in_vmem(same), in_vmem(other)), [IN_VMEM] * 2, (IN_VMEM,) * count)
+
+
+def land_kernel(same, other, *rest):
+    got, out = rest[:-1], rest[-1]
+    me = lax.axis_index("fsdp")
+    out[me] = same[0]
+    out[me ^ 1] = other[0]
+    for at, pieces in enumerate(got):
+        out[me ^ (2 * at + 2)] = pieces[0]
+        out[me ^ (2 * at + 3)] = pieces[1]
+
+
+def land(same, other, got):
+    out = pltpu.VMEM((2 * same.shape[0],) + same.shape[1:], same.dtype)
+    ins = [in_vmem(x) for x in (same, other, *got)]
+    return call(land_kernel, out, ins, [IN_VMEM] * len(ins), IN_VMEM)
+
+
+def assemble(whole, pieces):
+    slabs, rows, _ = pieces[0].shape
+    for slab in range(slabs):
+        for part, piece in enumerate(pieces):
+            at = (slab * len(pieces) + part) * rows
+            whole[at : at + rows, :] = piece[slab]
+
+
+def precondition(root, whole, right):
+    half = jnp.dot(root, whole[...], preferred_element_type=jnp.float32).astype(jnp.bfloat16)
+    return jnp.dot(half, right, preferred_element_type=jnp.float32)
+
+
+def own_rows(device, rows):
+    return pl.ds(pl.multiple_of(device * rows, rows), rows)
+
+
+def second_of(live, old, values):
+    return jnp.where(live, ADAM_BETA * old + (1.0 - ADAM_BETA) * values * values, old)
+
+
+def norms_of(precond, values, moment):
+    adam = values / (jnp.sqrt(moment) + EPSILON)
+    return jnp.sum(precond * precond), jnp.sum(adam * adam)
+
+
+def put_norms(kept, slot, sums):
+    row = lax.broadcasted_iota(jnp.int32, kept.shape, 0)
+    return jnp.where(row == 2 * slot, sums[0], jnp.where(row == 2 * slot + 1, sums[1], kept))
+
+
+class Writes:
+    def __init__(self, stage, sems):
+        self.stage, self.sems, self.copies = stage, sems, []
+
+    def put(self, value, out, slot):
+        at = len(self.copies)
+        self.stage[at] = value
+        self.copies.append(pltpu.make_async_copy(self.stage.at[at], out.at[slot], self.sems.at[at]))
+        self.copies[-1].start()
+
+    def wait(self):
+        for copy in self.copies:
+            copy.wait()
+
+
+def work_direct(slot, live, whole, root, right, moment, precond_out, moment_out, writes):
+    precond = precondition(root[slot], whole, right[slot])
+    if precond_out is not None:
+        precond_out[slot] = precond
+    values = whole[own_rows(lax.axis_index("dp"), root.shape[1]), :].astype(jnp.float32)
+    new = second_of(live, moment[slot], values)
+    writes.put(new, moment_out, slot)
+    return precond, values, new
+
+
+def work_gram(slot, live, whole, left, right, left_out, right_out, writes):
+    rows = own_rows(lax.axis_index("dp"), left.shape[1])
+    for part, dims, old, out in (
+        (whole[rows, :], ((1,), (1,)), left, left_out),
+        (whole[:, rows], ((0,), (0,)), right, right_out),
+    ):
+        term = lax.dot_general(part, whole[...], (dims, ((), ())), preferred_element_type=jnp.float32)
+        kept = old[slot]
+        writes.put(jnp.where(live, SHAMPOO_BETA * kept + (1.0 - SHAMPOO_BETA) * term, kept), out, slot)
+
+
+def own_kernel(ways, meta, a, b, root, right, moment, left, right_stats, lent, *rest):
+    precond_out, moment_out, norms, left_out, right_out, whole, stage, sems = rest
+    writes = Writes(stage, sems)
+    assemble(whole, (a, b))
+    slot, held = meta[0], meta[ways]
+    live = slot < held
+    sums = norms_of(*work_direct(slot, live, whole, root, right, moment, precond_out, moment_out, writes))
+    values = whole[own_rows(lax.axis_index("dp") ^ (ways - 1), root.shape[1]), :].astype(jnp.float32)
+    there = precondition(lent[0], whole, right[slot])
+    more = norms_of(there, values, second_of(live, lent[1].astype(jnp.float32), values))
+    norms[...] = put_norms(jnp.zeros(norms.shape, jnp.float32), slot, (sums[0] + more[0], sums[1] + more[1]))
+    work_gram(slot, live, whole, left, right_stats, left_out, right_out, writes)
+    writes.wait()
+
+
+def beside_kernel(ways, meta, a0, b0, a1, b1, root, right, moment, kept0, kept1, norms_in, *rest):
+    precond_out, moment_out, norms, whole, stage, sems = rest
+    writes = Writes(stage, sems)
+    total = norms_in[...]
+    for distance, pieces in ((1, (a0, b0)), (2, (a1, b1))):
+        assemble(whole.at[distance - 1], pieces)
+        slot = meta[distance]
+        live = slot < meta[ways]
+        got = work_direct(slot, live, whole.at[distance - 1], root, right, moment, precond_out, moment_out, writes)
+        total = put_norms(total, slot, norms_of(*got))
+    norms[...] = total
+    writes.wait()
+
+
+def gram_kernel(ways, meta, a0, b0, a1, b1, left, right_stats, kept0, kept1, *rest):
+    left_out, right_out, whole, stage, sems = rest
+    writes = Writes(stage, sems)
+    for distance, pieces in ((1, (a0, b0)), (2, (a1, b1))):
+        assemble(whole.at[distance - 1], pieces)
+        slot = meta[distance]
+        work_gram(
+            slot, slot < meta[ways], whole.at[distance - 1], left, right_stats, left_out, right_out, writes
+        )
+    writes.wait()
+
+
+def last_kernel(ways, meta, a, b, root, right, moment, left, right_stats, precond, *rest):
+    norms, rest = rest[:ways], rest[ways + 3 :]
+    update, moment_out, left_out, right_out, whole, stage, sems = rest
+    writes = Writes(stage, sems)
+    total = norms[0][...]
+    for part in norms[1:]:
+        total = total + part[...]
+    row = lax.broadcasted_iota(jnp.int32, total.shape, 0)
+
+    def scaled(value, slot):
+        live = slot < meta[ways]
+        pick = lambda at: jnp.sum(jnp.where(row == at, total, 0.0), axis=0, keepdims=True)[:, 0:1]
+        scale = jnp.where(live, jnp.sqrt(pick(2 * slot + 1) / jnp.where(live, pick(2 * slot), 1.0)), 0.0)
+        return jnp.where(live, value * scale, 0.0)
+
+    for distance in range(ways - 1):
+        slot = meta[distance]
+        writes.put(scaled(precond[slot], slot), update, slot)
+    assemble(whole, (a, b))
+    slot = meta[ways - 1]
+    live = slot < meta[ways]
+    value, _, _ = work_direct(slot, live, whole, root, right, moment, None, moment_out, writes)
+    writes.put(scaled(value, slot), update, slot)
+    work_gram(slot, live, whole, left, right_stats, left_out, right_out, writes)
+    writes.wait()
+
+
+def work(kernel, ways, meta, ins, kept, outs, staged, wholes):
+    width = ins[0].shape[-1]
+    rows = outs[0].shape[1]
+    args = [meta] + [in_vmem(x) for x in ins]
+    specs = [IN_SMEM] + [IN_VMEM] * len(ins)
+    alias = {}
+    for array, near, out in kept:
+        if out is not None:
+            alias[len(args)] = out
+        args.append(in_vmem(array) if near else in_hbm(array))
+        specs.append(IN_VMEM if near else IN_HBM)
+    spec_of = lambda ref: IN_HBM if ref.memory_space == pltpu.HBM else IN_VMEM
+    return call(
+        functools.partial(kernel, ways),
+        tuple(outs),
+        args,
+        specs,
+        tuple(spec_of(x) for x in outs),
+        [
+            VMEM((width, width) if wholes == 1 else (wholes, width, width), jnp.bfloat16),
+            VMEM((staged, rows, width), jnp.float32),
+            pltpu.SemaphoreType.DMA((staged,)),
+        ],
+        input_output_aliases=alias,
+    )
+
+
+def on_device_direct(
+    grads, left_stats, right_stats, left_root, right_root, second_moment, slot_block, counts
+):
+    ways, chunks = lax.axis_size("dp"), 2
+    owners, slots = slot_block.shape
+    first = (left_root[0], right_root[0], second_moment[0])
+    second = (left_stats[0], right_stats[0])
+    parts = []
+    for part in range(chunks):
+        dealt = deal(slot_block, counts, grads[0], ways, part, chunks)
+        parts.append(list(dealt[:1]))
+        for k in range(1, ways):
+            parts[part].append(exchange(dealt[k], "dp", k))
+    meta, lent = ready(counts, left_root[0], second_moment[0], ways)
+    lent = exchange(lent, "dp", ways - 1)
+    first = fetch(first)
+    second = fetch(second)
+    blocks = []
+    for part in range(chunks):
+        same, other = sort(counts, parts[part], owners)
+        other = exchange(other, "fsdp", 1)
+        sent = pair(same, other)
+        got = [None] * len(sent)
+        for k in range(len(sent)):
+            got[k] = exchange(sent[k], "fsdp", 2 * k + 2)
+        blocks.append(land(same, other, got))
+    side, over = [], []
+    for part in range(chunks):
+        side.append(exchange(blocks[part], "dp", 1))
+        over.append(exchange(blocks[part], "dp", 2))
+    relay0 = exchange(side[0], "dp", 2)
+    relay1 = exchange(over[1], "dp", 1)
+
+    state = (slots,) + left_stats.shape[2:]
+    near, far = pltpu.VMEM(state, jnp.float32), pltpu.HBM(state, jnp.float32)
+    norm = pltpu.VMEM((-(-2 * slots // 8) * 8, 128), jnp.float32)
+    ins = (*blocks, *first, *second, lent)
+    precond, moment, norms, left, right = work(own_kernel, ways, meta, ins, (), (near, far, norm, far, far), 3, 1)
+    kept = ((precond, True, 0), (moment, False, 1), (norms, True, None))
+    precond, moment, norms = work(beside_kernel, ways, meta, (*side, *over, *first), kept, (near, far, norm), 2, 2)
+    all_norms = [norms]
+    for k in range(1, ways):
+        all_norms.append(exchange(norms, "dp", k))
+    kept = ((left, False, 0), (right, False, 1))
+    left, right = work(gram_kernel, ways, meta, (*side, *over, *second), kept, (far, far), 4, 2)
+    ins = (relay0, relay1, *first, *second, precond, *all_norms)
+    kept = ((moment, False, 1), (left, False, 2), (right, False, 3))
+    update, second_new, left_new, right_new = work(last_kernel, ways, meta, ins, kept, (far,) * 4, ways + 3, 1)
+    return (left_new[None], right_new[None], second_new[None], update[None])
 
 
 def on_device(
@@ -86,6 +497,14 @@
         P("fsdp", None, "dp", None),
         P("fsdp", None, "dp", None),
     )
-    return jax.shard_map(
-        on_device, mesh=mesh, in_specs=in_specs, out_specs=out_specs, check_vma=False
-    )
+
+    ways, owners = mesh.shape["dp"], mesh.shape["fsdp"]
+    square = ways == 4 and owners % 2 == 0 and owners & (owners - 1) == 0
+
+    def fits(args):
+        return square and args[6].shape[1] == ways and args[0].shape[1] % ways == 0
+
+    def body(*args):
+        return (on_device_direct if fits(args) else on_device)(*args)
+
+    return jax.shard_map(body, mesh=mesh, in_specs=in_specs, out_specs=out_specs, check_vma=False)

time: 134 us -> 66.5 us (0.50)
  waiting for transfers between devices: 63.7 us -> 15 us
  starting transfers between devices: 0.08 us -> 30.2 us
  blocking collectives: 28.7 us -> 0 us
  Pallas kernels: 0 us -> 20.1 us
  local copies, waits for them, and re-layouts: 14.5 us -> 0 us
  between operations: 14.1 us -> 0.79 us
  matrix products: 6.24 us -> 0 us
  other arithmetic: 5.99 us -> 0 us
    all_gather x1 -> x0, waiting for transfers between devices: 32 us -> none  [on_device(): gathered = lax.all_gather(received, 'dp', axis=2, tiled=True)]
    reduce_scatter x1 -> x0, waiting for transfers between devices: 31.7 us -> none  [on_device(): lax.psum_scatter(flat_partial.astype(jnp.bfloat16), 'dp', scatter_dimensi...]
    ppermute x0 -> x24, starting transfers between devices: none -> 30.2 us  [exchange(): return lax.ppermute(value, axis, [(i, i ^ distance) for i in range(size)])]
    pallas_call x0 -> x15, Pallas kernels: none -> 20.1 us  [call(): pl.pallas_call(kernel, out_shape=out, in_specs=in_specs, out_specs=out_sp...]
    all_to_all x1 -> x0, blocking collectives: 19.8 us -> none  [on_device(): lax.all_to_all(picked, 'fsdp', split_axis=0, concat_axis=1, tiled=True)]
    ppermute x0 -> x24, waiting for transfers between devices: none -> 15 us  [exchange(): return lax.ppermute(value, axis, [(i, i ^ distance) for i in range(size)])]
    psum x1 -> x0, blocking collectives: 8.93 us -> none  [on_device(): lax.psum((jnp.sum(precond * precond, axis=(1, 2)), jnp.sum(adam * adam, a...]
    dot_general x3 -> x0, matrix products: 6.24 us -> none  [the longest x1 2.93 us: on_device(): jnp.einsum('crk,ckj->crj', left_half, right_root[0], preferred_element_ty...]
  transfers between devices with their start and end apart: 2 -> 24, of which waited for: 2 -> 9; matrix products, arithmetic and copies ran while one was open for 1% -> 0% of each run, Pallas kernels for 0% -> 24%
where the time goes in v1:
time: 66.5 us; the launch traced here: 66.1 us
  starting transfers between devices  30.2 us (45%)
  Pallas kernels  20.1 us (30%)
  waiting for transfers between devices  15 us (23%)
  between operations  0.79 us (1%)
    ppermute x24, starting transfers between devices, exchange(): return lax.ppermute(value, axis, [(i, i ^ distance) for i in range(size)])  30.2 us
    pallas_call x15, Pallas kernels, call(): pl.pallas_call(kernel, out_shape=out, in_specs=in_specs, out_specs=out_sp...  20.1 us
    ppermute x24, waiting for transfers between devices, exchange(): return lax.ppermute(value, axis, [(i, i ^ distance) for i in range(size)])  15 us
  transfers between devices with their start and end apart: 24, of which 9 were waited for; matrix products, arithmetic and copies ran while one was open for 0% of the time, Pallas kernels for 24%

profile of v1, /device:TPU:0, one launch (start us, length us, event | category | flops | bytes accessed | tf_op | source)
XLA Modules:
  0.0 66.1 jit_solution(1870401986303620113)
XLA Ops:
  0.6 1.9 %shard_map.116 = (bf16[4,32,512]{2,1,0:T(8,128)(2,1)S(1)}, bf16[4,32,512]{2,1,0:T(8,128)(2,1)S(1)}, bf16[4,32,512]{2,1,0:T(8,128)(2,1)S(1)}, bf16[4,32,512]{2,1,0:T(8,128)(2,1)S(1)}) custom-call(s32[4,8]{1,0:T(4,128)} %bitcast.23, s32[8]{0:T(128)} %counts.9, bf16[16,64,512]{2,1,0:T(8,128)(2,1)} %bitcast.13), custom_call_target="tpu_custom_call" | custom-call | flops 10000000 | bytes 1000000 | tf_op jit(solution)/shard_map/pallas_call | solution.py:33
  2.5 3.0 %collective-permute-start.9 = (bf16[4,32,512]{2,1,0:T(8,128)(2,1)S(1)}, bf16[4,32,512]{2,1,0:T(8,128)(2,1)S(1)}, u32[]{:S(2)}, u32[]{:S(2)}) collective-permute-start(bf16[4,32,512]{2,1,0:T(8,128)(2,1)S(1)} %get-tuple-element.54), channel_id=1, source_target_pairs={{0,8},{8,0},{16,24},{24,16},{1,9},{9,1},{17,25},{25,17},{2,10},{10... | collective-permute-start | bytes 393224 | tf_op jit(solution)/shard_map/ppermute | solution.py:21
  5.6 1.5 %collective-permute-start.10 = (bf16[4,32,512]{2,1,0:T(8,128)(2,1)S(1)}, bf16[4,32,512]{2,1,0:T(8,128)(2,1)S(1)}, u32[]{:S(2)}, u32[]{:S(2)}) collective-permute-start(bf16[4,32,512]{2,1,0:T(8,128)(2,1)S(1)} %get-tuple-element.55), channel_id=1, source_target_pairs={{0,16},{8,24},{16,0},{24,8},{1,17},{9,25},{17,1},{25,9},{2,18},{10... | collective-permute-start | bytes 393224 | tf_op jit(solution)/shard_map/ppermute | solution.py:21
  7.1 1.9 %shard_map.112 = (bf16[4,32,512]{2,1,0:T(8,128)(2,1)S(1)}, bf16[4,32,512]{2,1,0:T(8,128)(2,1)S(1)}, bf16[4,32,512]{2,1,0:T(8,128)(2,1)S(1)}, bf16[4,32,512]{2,1,0:T(8,128)(2,1)S(1)}) custom-call(s32[4,8]{1,0:T(4,128)} %bitcast.24, s32[8]{0:T(128)} %counts.9, bf16[16,64,512]{2,1,0:T(8,128)(2,1)} %bitcast.14), custom_call_target="tpu_custom_call" | custom-call | flops 10000000 | bytes 1000000 | tf_op jit(solution)/shard_map/pallas_call | solution.py:33
  9.0 2.0 %collective-permute-start = (bf16[4,32,512]{2,1,0:T(8,128)(2,1)S(1)}, bf16[4,32,512]{2,1,0:T(8,128)(2,1)S(1)}, u32[]{:S(2)}, u32[]{:S(2)}) collective-permute-start(bf16[4,32,512]{2,1,0:T(8,128)(2,1)S(1)} %get-tuple-element.45), channel_id=1, source_target_pairs={{0,8},{8,0},{16,24},{24,16},{1,9},{9,1},{17,25},{25,17},{2,10},{10... | collective-permute-start | bytes 393224 | tf_op jit(solution)/shard_map/ppermute | solution.py:21
  11.0 1.5 %collective-permute-start.1 = (bf16[4,32,512]{2,1,0:T(8,128)(2,1)S(1)}, bf16[4,32,512]{2,1,0:T(8,128)(2,1)S(1)}, u32[]{:S(2)}, u32[]{:S(2)}) collective-permute-start(bf16[4,32,512]{2,1,0:T(8,128)(2,1)S(1)} %get-tuple-element.46), channel_id=1, source_target_pairs={{0,16},{8,24},{16,0},{24,8},{1,17},{9,25},{17,1},{25,9},{2,18},{10... | collective-permute-start | bytes 393224 | tf_op jit(solution)/shard_map/ppermute | solution.py:21
  12.9 1.2 %collective-permute-done.11.rest_3_ = bf16[4,32,512]{2,1,0:T(8,128)(2,1)S(1)} collective-permute-done((bf16[4,32,512]{2,1,0:T(8,128)(2,1)S(1)}, bf16[4,32,512]{2,1,0:T(8,128)(2,1)S(1)}, u32[]{:S(2)}, u32[]{:S(2)}) %collective-permute-start.11) | collective-permute-done | bytes 131104 | tf_op jit(solution)/shard_map/ppermute | solution.py:21
  15.9 3.1 %collective-permute-done.1.rest_2_ = bf16[4,32,512]{2,1,0:T(8,128)(2,1)S(1)} collective-permute-done((bf16[4,32,512]{2,1,0:T(8,128)(2,1)S(1)}, bf16[4,32,512]{2,1,0:T(8,128)(2,1)S(1)}, u32[]{:S(2)}, u32[]{:S(2)}) %collective-permute-start.1) | collective-permute-done | bytes 131104 | tf_op jit(solution)/shard_map/ppermute | solution.py:21
  19.0 0.8 %shard_map.113 = (bf16[4,32,512]{2,1,0:T(8,128)(2,1)S(1)}, bf16[4,32,512]{2,1,0:T(8,128)(2,1)S(1)}) custom-call(s32[8]{0:T(128)} %counts.9, bf16[4,32,512]{2,1,0:T(8,128)(2,1)S(1)} %get-tuple-element.44.rest_0_, bf16[4,32,512]{2,1,0:T(8,128)(2,1)S(1)} %collective-permute-done.rest_1_, bf16[4,32,512]{2,1,0:T(8,128)(2,1)S(1)} %collective-permute-done.1.rest_2_, ...), custom_call_target="tpu_custom_call" | custom-call | flops 10000000 | bytes 1000000 | tf_op jit(solution)/shard_map/pallas_call | solution.py:33
  19.9 1.6 %collective-permute-start.13 = (bf16[2,32,512]{2,1,0:T(8,128)(2,1)S(1)}, bf16[2,32,512]{2,1,0:T(8,128)(2,1)S(1)}, u32[]{:S(2)}, u32[]{:S(2)}) collective-permute-start(bf16[2,32,512]{2,1,0:T(8,128)(2,1)S(1)} %get-tuple-element.59), channel_id=1, source_target_pairs={{0,2},{1,3},{2,0},{3,1},{4,6},{5,7},{6,4},{7,5},{8,10},{9,11},{10,... | collective-permute-start | bytes 196616 | tf_op jit(solution)/shard_map/ppermute | solution.py:21
  21.6 2.6 %collective-permute-start.14 = (bf16[2,32,512]{2,1,0:T(8,128)(2,1)S(1)}, bf16[2,32,512]{2,1,0:T(8,128)(2,1)S(1)}, u32[]{:S(2)}, u32[]{:S(2)}) collective-permute-start(bf16[2,32,512]{2,1,0:T(8,128)(2,1)S(1)} %get-tuple-element.60), channel_id=1, source_target_pairs={{0,4},{1,5},{2,6},{3,7},{4,0},{5,1},{6,2},{7,3},{8,12},{9,13},{10,... | collective-permute-start | bytes 196616 | tf_op jit(solution)/shard_map/ppermute | solution.py:21
  25.1 3.5 %collective-permute-start.5 = (bf16[2,32,512]{2,1,0:T(8,128)(2,1)S(1)}, bf16[2,32,512]{2,1,0:T(8,128)(2,1)S(1)}, u32[]{:S(2)}, u32[]{:S(2)}) collective-permute-start(bf16[2,32,512]{2,1,0:T(8,128)(2,1)S(1)} %get-tuple-element.51), channel_id=1, source_target_pairs={{0,4},{1,5},{2,6},{3,7},{4,0},{5,1},{6,2},{7,3},{8,12},{9,13},{10,... | collective-permute-start | bytes 196616 | tf_op jit(solution)/shard_map/ppermute | solution.py:21
  29.0 2.0 %collective-permute-done.15.rest_2_ = bf16[2,32,512]{2,1,0:T(8,128)(2,1)S(1)} collective-permute-done((bf16[2,32,512]{2,1,0:T(8,128)(2,1)S(1)}, bf16[2,32,512]{2,1,0:T(8,128)(2,1)S(1)}, u32[]{:S(2)}, u32[]{:S(2)}) %collective-permute-start.15) | collective-permute-done | bytes 65568 | tf_op jit(solution)/shard_map/ppermute | solution.py:21
  30.9 1.6 %collective-permute-start.16 = (bf16[8,32,512]{2,1,0:T(8,128)(2,1)S(1)}, bf16[8,32,512]{2,1,0:T(8,128)(2,1)S(1)}, u32[]{:S(2)}, u32[]{:S(2)}) collective-permute-start(bf16[8,32,512]{2,1,0:T(8,128)(2,1)S(1)} %shard_map.119.b), channel_id=1, source_target_pairs={{0,16},{8,24},{16,0},{24,8},{1,17},{9,25},{17,1},{25,9},{2,18},{10... | collective-permute-start | bytes 786440 | tf_op jit(solution)/shard_map/ppermute | solution.py:21
  32.5 3.1 %collective-permute-done.5.rest_1_ = bf16[2,32,512]{2,1,0:T(8,128)(2,1)S(1)} collective-permute-done((bf16[2,32,512]{2,1,0:T(8,128)(2,1)S(1)}, bf16[2,32,512]{2,1,0:T(8,128)(2,1)S(1)}, u32[]{:S(2)}, u32[]{:S(2)}) %collective-permute-start.5) | collective-permute-done | bytes 65568 | tf_op jit(solution)/shard_map/ppermute | solution.py:21
  35.6 1.3 %collective-permute-start.7 = (bf16[8,32,512]{2,1,0:T(8,128)(2,1)S(1)}, bf16[8,32,512]{2,1,0:T(8,128)(2,1)S(1)}, u32[]{:S(2)}, u32[]{:S(2)}) collective-permute-start(bf16[8,32,512]{2,1,0:T(8,128)(2,1)S(1)} %shard_map.115.a), channel_id=1, source_target_pairs={{0,8},{8,0},{16,24},{24,16},{1,9},{9,1},{17,25},{25,17},{2,10},{10... | collective-permute-start | bytes 786440 | tf_op jit(solution)/shard_map/ppermute | solution.py:21
  36.9 2.3 %shard_map.111 = (s32[5]{0:T(128)S(1)}, bf16[2,128,512]{2,1,0:T(8,128)(2,1)S(1)}) custom-call(s32[8]{0:T(128)} %counts.9, bf16[4,128,512]{2,1,0:T(8,128)(2,1)} %bitcast.19, f32[4,128,512]{2,1,0:T(8,128)} %bitcast.11), custom_call_target="tpu_custom_call" | custom-call | flops 10000000 | bytes 1000000 | tf_op jit(solution)/shard_map/pallas_call | solution.py:33
  39.2 1.8 %collective-permute-start.20 = (bf16[2,128,512]{2,1,0:T(8,128)(2,1)S(1)}, bf16[2,128,512]{2,1,0:T(8,128)(2,1)S(1)}, u32[]{:S(2)}, u32[]{:S(2)}) collective-permute-start(bf16[2,128,512]{2,1,0:T(8,128)(2,1)S(1)} %get-tuple-element.67), channel_id=1, source_target_pairs={{0,24},{8,16},{16,8},{24,0},{1,25},{9,17},{17,9},{25,1},{2,26},{10... | collective-permute-start | bytes 786440 | tf_op jit(solution)/shard_map/ppermute | solution.py:21
  41.6 1.2 %collective-permute-start.19 = (bf16[8,32,512]{2,1,0:T(8,128)(2,1)S(1)}, bf16[8,32,512]{2,1,0:T(8,128)(2,1)S(1)}, u32[]{:S(2)}, u32[]{:S(2)}) collective-permute-start(bf16[8,32,512]{2,1,0:T(8,128)(2,1)S(1)} %shard_map.115.a), channel_id=1, source_target_pairs={{0,16},{8,24},{16,0},{24,8},{1,17},{9,25},{17,1},{25,9},{2,18},{10... | collective-permute-start | bytes 786440 | tf_op jit(solution)/shard_map/ppermute | solution.py:21
  43.6 0.8 %collective-permute-done.7.a0 = bf16[8,32,512]{2,1,0:T(8,128)(2,1)S(1)} collective-permute-done((bf16[8,32,512]{2,1,0:T(8,128)(2,1)S(1)}, bf16[8,32,512]{2,1,0:T(8,128)(2,1)S(1)}, u32[]{:S(2)}, u32[]{:S(2)}) %collective-permute-start.7) | collective-permute-done | bytes 262176 | tf_op jit(solution)/shard_map/ppermute | solution.py:21
  44.4 1.8 %collective-permute-start.8 = (bf16[8,32,512]{2,1,0:T(8,128)(2,1)S(1)}, bf16[8,32,512]{2,1,0:T(8,128)(2,1)S(1)}, u32[]{:S(2)}, u32[]{:S(2)}) collective-permute-start(bf16[8,32,512]{2,1,0:T(8,128)(2,1)S(1)} %collective-permute-done.7.a0), channel_id=1, source_target_pairs={{0,16},{8,24},{16,0},{24,8},{1,17},{9,25},{17,1},{25,9},{2,18},{10... | collective-permute-start | bytes 786440 | tf_op jit(solution)/shard_map/ppermute | solution.py:21
  46.3 2.0 %shard_map.120 = (bf16[4,128,512]{2,1,0:T(8,128)(2,1)S(1)}, bf16[4,512,512]{2,1,0:T(8,128)(2,1)S(1)}, f32[4,128,512]{2,1,0:T(8,128)S(1)}) custom-call(bf16[4,128,512]{2,1,0:T(8,128)(2,1)} %bitcast.20, bf16[4,512,512]{2,1,0:T(8,128)(2,1)} %bitcast.18, f32[4,128,512]{2,1,0:T(8,128)} %bitcast.12), custom_call_target="tpu_custom_call" | custom-call | flops 10000000 | bytes 1000000 | tf_op jit(solution)/shard_map/pallas_call | solution.py:33
  48.3 1.6 %shard_map.121 = (f32[4,128,512]{2,1,0:T(8,128)S(1)}, f32[4,128,512]{2,1,0:T(8,128)S(1)}) custom-call(f32[4,128,512]{2,1,0:T(8,128)} %bitcast.21, f32[4,128,512]{2,1,0:T(8,128)} %bitcast.22), custom_call_target="tpu_custom_call" | custom-call | flops 10000000 | bytes 1000000 | tf_op jit(solution)/shard_map/pallas_call | solution.py:33
  49.9 1.5 %collective-permute-done.20.lent = bf16[2,128,512]{2,1,0:T(8,128)(2,1)S(1)} collective-permute-done((bf16[2,128,512]{2,1,0:T(8,128)(2,1)S(1)}, bf16[2,128,512]{2,1,0:T(8,128)(2,1)S(1)}, u32[]{:S(2)}, u32[]{:S(2)}) %collective-permute-start.20) | collective-permute-done | bytes 262176 | tf_op jit(solution)/shard_map/ppermute | solution.py:21
  51.4 2.5 %shard_map.122 = (f32[4,128,512]{2,1,0:T(8,128)S(1)}, f32[4,128,512]{2,1,0:T(8,128)}, f32[8,128]{1,0:T(8,128)S(1)}, f32[4,128,512]{2,1,0:T(8,128)}, f32[4,128,512]{2,1,0:T(8,128)}) custom-call(s32[5]{0:T(128)S(1)} %get-tuple-element.43.meta, bf16[8,32,512]{2,1,0:T(8,128)(2,1)S(1)} %shard_map.115.a, bf16[8,32,512]{2,1,0:T(8,128)(2,1)S(1)} %shard_map.119.b, ...), custom_call_target="tpu_custom_call" | custom-call | flops 10000000 | bytes 1000000 | tf_op jit(solution)/shard_map/pallas_call | solution.py:33
  53.8 1.9 %collective-permute-done.18.b0 = bf16[8,32,512]{2,1,0:T(8,128)(2,1)S(1)} collective-permute-done((bf16[8,32,512]{2,1,0:T(8,128)(2,1)S(1)}, bf16[8,32,512]{2,1,0:T(8,128)(2,1)S(1)}, u32[]{:S(2)}, u32[]{:S(2)}) %collective-permute-start.18) | collective-permute-done | bytes 262176 | tf_op jit(solution)/shard_map/ppermute | solution.py:21
  55.7 2.0 %shard_map.123 = (f32[4,128,512]{2,1,0:T(8,128)S(1)}, f32[4,128,512]{2,1,0:T(8,128)}, f32[8,128]{1,0:T(8,128)S(1)}) custom-call(s32[5]{0:T(128)S(1)} %get-tuple-element.43.meta, bf16[8,32,512]{2,1,0:T(8,128)(2,1)S(1)} %collective-permute-done.7.a0, bf16[8,32,512]{2,1,0:T(8,128)(2,1)S(1)} %collective-permute-done.18.b0, ...), custom_call_target="tpu_custom_call", output_to_operand_aliasing={{0}: (8, {}), {1}: (9, {})} | custom-call | flops 10000000 | bytes 1000000 | tf_op jit(solution)/shard_map/pallas_call | solution.py:33
  57.8 1.6 %collective-permute-start.23 = (f32[8,128]{1,0:T(8,128)S(1)}, f32[8,128]{1,0:T(8,128)S(1)}, u32[]{:S(2)}, u32[]{:S(2)}) collective-permute-start(f32[8,128]{1,0:T(8,128)S(1)} %get-tuple-element.72.rest_0_), channel_id=1, source_target_pairs={{0,24},{8,16},{16,8},{24,0},{1,25},{9,17},{17,9},{25,1},{2,26},{10... | collective-permute-start | bytes 12296 | tf_op jit(solution)/shard_map/ppermute | solution.py:21
  59.4 0.9 %collective-permute-start.22 = (f32[8,128]{1,0:T(8,128)S(1)}, f32[8,128]{1,0:T(8,128)S(1)}, u32[]{:S(2)}, u32[]{:S(2)}) collective-permute-start(f32[8,128]{1,0:T(8,128)S(1)} %get-tuple-element.72.rest_0_), channel_id=1, source_target_pairs={{0,16},{8,24},{16,0},{24,8},{1,17},{9,25},{17,1},{25,9},{2,18},{10... | collective-permute-start | bytes 12296 | tf_op jit(solution)/shard_map/ppermute | solution.py:21
  60.3 1.1 %collective-permute-start.21 = (f32[8,128]{1,0:T(8,128)S(1)}, f32[8,128]{1,0:T(8,128)S(1)}, u32[]{:S(2)}, u32[]{:S(2)}) collective-permute-start(f32[8,128]{1,0:T(8,128)S(1)} %get-tuple-element.72.rest_0_), channel_id=1, source_target_pairs={{0,8},{8,0},{16,24},{24,16},{1,9},{9,1},{17,25},{25,17},{2,10},{10... | collective-permute-start | bytes 12296 | tf_op jit(solution)/shard_map/ppermute | solution.py:21
  61.3 2.0 %shard_map.124 = (f32[4,128,512]{2,1,0:T(8,128)}, f32[4,128,512]{2,1,0:T(8,128)}) custom-call(s32[5]{0:T(128)S(1)} %get-tuple-element.43.meta, bf16[8,32,512]{2,1,0:T(8,128)(2,1)S(1)} %collective-permute-done.7.a0, bf16[8,32,512]{2,1,0:T(8,128)(2,1)S(1)} %collective-permute-done.18.b0, ...), custom_call_target="tpu_custom_call", output_to_operand_aliasing={{0}: (7, {}), {1}: (8, {})} | custom-call | flops 10000000 | bytes 1000000 | tf_op jit(solution)/shard_map/pallas_call | solution.py:33
  63.9 2.2 %shard_map.125 = (f32[4,128,512]{2,1,0:T(8,128)}, f32[4,128,512]{2,1,0:T(8,128)}, f32[4,128,512]{2,1,0:T(8,128)}, f32[4,128,512]{2,1,0:T(8,128)}) custom-call(s32[5]{0:T(128)S(1)} %get-tuple-element.43.meta, bf16[8,32,512]{2,1,0:T(8,128)(2,1)S(1)} %collective-permute-done.8.a, ...), custom_call_target="tpu_custom_call", output_to_operand_aliasing={{1}: (13, {}), {2}: (14, {}), {3}: (15, {})} | custom-call | flops 10000000 | bytes 1000000 | tf_op jit(solution)/shard_map/pallas_call | solution.py:33
  (31 shorter events, 5.4 us)
Async XLA Ops:
  2.5 10.0 %collective-permute-start.9 = (bf16[4,32,512]{2,1,0:T(8,128)(2,1)S(1)}, bf16[4,32,512]{2,1,0:T(8,128)(2,1)S(1)}, u32[]{:S(2)}, u32[]{:S(2)}) collective-permute-start(bf16[4,32,512]{2,1,0:T(8,128)(2,1)S(1)} %get-tuple-element.54), channel_id=1, source_target_pairs={{0,8},{8,0},{16,24},{24,16},{1,9},{9,1},{17,25},{25,17},{2,10},{10... | collective-permute-start | bytes 393224 | tf_op jit(solution)/shard_map/ppermute | solution.py:21
  5.6 7.4 %collective-permute-start.10 = (bf16[4,32,512]{2,1,0:T(8,128)(2,1)S(1)}, bf16[4,32,512]{2,1,0:T(8,128)(2,1)S(1)}, u32[]{:S(2)}, u32[]{:S(2)}) collective-permute-start(bf16[4,32,512]{2,1,0:T(8,128)(2,1)S(1)} %get-tuple-element.55), channel_id=1, source_target_pairs={{0,16},{8,24},{16,0},{24,8},{1,17},{9,25},{17,1},{25,9},{2,18},{10... | collective-permute-start | bytes 393224 | tf_op jit(solution)/shard_map/ppermute | solution.py:21
  7.1 7.1 %collective-permute-start.11 = (bf16[4,32,512]{2,1,0:T(8,128)(2,1)S(1)}, bf16[4,32,512]{2,1,0:T(8,128)(2,1)S(1)}, u32[]{:S(2)}, u32[]{:S(2)}) collective-permute-start(bf16[4,32,512]{2,1,0:T(8,128)(2,1)S(1)} %get-tuple-element.56), channel_id=1, source_target_pairs={{0,24},{8,16},{16,8},{24,0},{1,25},{9,17},{17,9},{25,1},{2,26},{10... | collective-permute-start | bytes 393224 | tf_op jit(solution)/shard_map/ppermute | solution.py:21
  9.0 6.9 %collective-permute-start = (bf16[4,32,512]{2,1,0:T(8,128)(2,1)S(1)}, bf16[4,32,512]{2,1,0:T(8,128)(2,1)S(1)}, u32[]{:S(2)}, u32[]{:S(2)}) collective-permute-start(bf16[4,32,512]{2,1,0:T(8,128)(2,1)S(1)} %get-tuple-element.45), channel_id=1, source_target_pairs={{0,8},{8,0},{16,24},{24,16},{1,9},{9,1},{17,25},{25,17},{2,10},{10... | collective-permute-start | bytes 393224 | tf_op jit(solution)/shard_map/ppermute | solution.py:21
  11.0 7.9 %collective-permute-start.1 = (bf16[4,32,512]{2,1,0:T(8,128)(2,1)S(1)}, bf16[4,32,512]{2,1,0:T(8,128)(2,1)S(1)}, u32[]{:S(2)}, u32[]{:S(2)}) collective-permute-start(bf16[4,32,512]{2,1,0:T(8,128)(2,1)S(1)} %get-tuple-element.46), channel_id=1, source_target_pairs={{0,16},{8,24},{16,0},{24,8},{1,17},{9,25},{17,1},{25,9},{2,18},{10... | collective-permute-start | bytes 393224 | tf_op jit(solution)/shard_map/ppermute | solution.py:21
  12.5 6.4 %collective-permute-start.2 = (bf16[4,32,512]{2,1,0:T(8,128)(2,1)S(1)}, bf16[4,32,512]{2,1,0:T(8,128)(2,1)S(1)}, u32[]{:S(2)}, u32[]{:S(2)}) collective-permute-start(bf16[4,32,512]{2,1,0:T(8,128)(2,1)S(1)} %get-tuple-element.47), channel_id=1, source_target_pairs={{0,24},{8,16},{16,8},{24,0},{1,25},{9,17},{17,9},{25,1},{2,26},{10... | collective-permute-start | bytes 393224 | tf_op jit(solution)/shard_map/ppermute | solution.py:21
  15.0 4.9 %collective-permute-start.12 = (bf16[4,32,512]{2,1,0:T(8,128)(2,1)S(1)}, bf16[4,32,512]{2,1,0:T(8,128)(2,1)S(1)}, u32[]{:S(2)}, u32[]{:S(2)}) collective-permute-start(bf16[4,32,512]{2,1,0:T(8,128)(2,1)S(1)} %get-tuple-element.58), channel_id=1, source_target_pairs={{0,1},{1,0},{2,3},{3,2},{4,5},{5,4},{6,7},{7,6},{8,9},{9,8},{10,11... | collective-permute-start | bytes 393224 | tf_op jit(solution)/shard_map/ppermute | solution.py:21
  19.8 4.6 %collective-permute-start.3 = (bf16[4,32,512]{2,1,0:T(8,128)(2,1)S(1)}, bf16[4,32,512]{2,1,0:T(8,128)(2,1)S(1)}, u32[]{:S(2)}, u32[]{:S(2)}) collective-permute-start(bf16[4,32,512]{2,1,0:T(8,128)(2,1)S(1)} %get-tuple-element.49), channel_id=1, source_target_pairs={{0,1},{1,0},{2,3},{3,2},{4,5},{5,4},{6,7},{7,6},{8,9},{9,8},{10,11... | collective-permute-start | bytes 393224 | tf_op jit(solution)/shard_map/ppermute | solution.py:21
  19.9 8.7 %collective-permute-start.13 = (bf16[2,32,512]{2,1,0:T(8,128)(2,1)S(1)}, bf16[2,32,512]{2,1,0:T(8,128)(2,1)S(1)}, u32[]{:S(2)}, u32[]{:S(2)}) collective-permute-start(bf16[2,32,512]{2,1,0:T(8,128)(2,1)S(1)} %get-tuple-element.59), channel_id=1, source_target_pairs={{0,2},{1,3},{2,0},{3,1},{4,6},{5,7},{6,4},{7,5},{8,10},{9,11},{10,... | collective-permute-start | bytes 196616 | tf_op jit(solution)/shard_map/ppermute | solution.py:21
  21.6 7.4 %collective-permute-start.14 = (bf16[2,32,512]{2,1,0:T(8,128)(2,1)S(1)}, bf16[2,32,512]{2,1,0:T(8,128)(2,1)S(1)}, u32[]{:S(2)}, u32[]{:S(2)}) collective-permute-start(bf16[2,32,512]{2,1,0:T(8,128)(2,1)S(1)} %get-tuple-element.60), channel_id=1, source_target_pairs={{0,4},{1,5},{2,6},{3,7},{4,0},{5,1},{6,2},{7,3},{8,12},{9,13},{10,... | collective-permute-start | bytes 196616 | tf_op jit(solution)/shard_map/ppermute | solution.py:21
  24.2 6.8 %collective-permute-start.15 = (bf16[2,32,512]{2,1,0:T(8,128)(2,1)S(1)}, bf16[2,32,512]{2,1,0:T(8,128)(2,1)S(1)}, u32[]{:S(2)}, u32[]{:S(2)}) collective-permute-start(bf16[2,32,512]{2,1,0:T(8,128)(2,1)S(1)} %get-tuple-element.61), channel_id=1, source_target_pairs={{0,6},{1,7},{2,4},{3,5},{4,2},{5,3},{6,0},{7,1},{8,14},{9,15},{10,... | collective-permute-start | bytes 196616 | tf_op jit(solution)/shard_map/ppermute | solution.py:21
  24.4 8.1 %collective-permute-start.4 = (bf16[2,32,512]{2,1,0:T(8,128)(2,1)S(1)}, bf16[2,32,512]{2,1,0:T(8,128)(2,1)S(1)}, u32[]{:S(2)}, u32[]{:S(2)}) collective-permute-start(bf16[2,32,512]{2,1,0:T(8,128)(2,1)S(1)} %get-tuple-element.50), channel_id=1, source_target_pairs={{0,2},{1,3},{2,0},{3,1},{4,6},{5,7},{6,4},{7,5},{8,10},{9,11},{10,... | collective-permute-start | bytes 196616 | tf_op jit(solution)/shard_map/ppermute | solution.py:21
  25.1 10.4 %collective-permute-start.5 = (bf16[2,32,512]{2,1,0:T(8,128)(2,1)S(1)}, bf16[2,32,512]{2,1,0:T(8,128)(2,1)S(1)}, u32[]{:S(2)}, u32[]{:S(2)}) collective-permute-start(bf16[2,32,512]{2,1,0:T(8,128)(2,1)S(1)} %get-tuple-element.51), channel_id=1, source_target_pairs={{0,4},{1,5},{2,6},{3,7},{4,0},{5,1},{6,2},{7,3},{8,12},{9,13},{10,... | collective-permute-start | bytes 196616 | tf_op jit(solution)/shard_map/ppermute | solution.py:21
  28.6 7.0 %collective-permute-start.6 = (bf16[2,32,512]{2,1,0:T(8,128)(2,1)S(1)}, bf16[2,32,512]{2,1,0:T(8,128)(2,1)S(1)}, u32[]{:S(2)}, u32[]{:S(2)}) collective-permute-start(bf16[2,32,512]{2,1,0:T(8,128)(2,1)S(1)} %get-tuple-element.52), channel_id=1, source_target_pairs={{0,6},{1,7},{2,4},{3,5},{4,2},{5,3},{6,0},{7,1},{8,14},{9,15},{10,... | collective-permute-start | bytes 196616 | tf_op jit(solution)/shard_map/ppermute | solution.py:21
  30.9 11.9 %collective-permute-start.16 = (bf16[8,32,512]{2,1,0:T(8,128)(2,1)S(1)}, bf16[8,32,512]{2,1,0:T(8,128)(2,1)S(1)}, u32[]{:S(2)}, u32[]{:S(2)}) collective-permute-start(bf16[8,32,512]{2,1,0:T(8,128)(2,1)S(1)} %shard_map.119.b), channel_id=1, source_target_pairs={{0,16},{8,24},{16,0},{24,8},{1,17},{9,25},{17,1},{25,9},{2,18},{10... | collective-permute-start | bytes 786440 | tf_op jit(solution)/shard_map/ppermute | solution.py:21
  35.6 8.8 %collective-permute-start.7 = (bf16[8,32,512]{2,1,0:T(8,128)(2,1)S(1)}, bf16[8,32,512]{2,1,0:T(8,128)(2,1)S(1)}, u32[]{:S(2)}, u32[]{:S(2)}) collective-permute-start(bf16[8,32,512]{2,1,0:T(8,128)(2,1)S(1)} %shard_map.115.a), channel_id=1, source_target_pairs={{0,8},{8,0},{16,24},{24,16},{1,9},{9,1},{17,25},{25,17},{2,10},{10... | collective-permute-start | bytes 786440 | tf_op jit(solution)/shard_map/ppermute | solution.py:21
  39.2 12.1 %collective-permute-start.20 = (bf16[2,128,512]{2,1,0:T(8,128)(2,1)S(1)}, bf16[2,128,512]{2,1,0:T(8,128)(2,1)S(1)}, u32[]{:S(2)}, u32[]{:S(2)}) collective-permute-start(bf16[2,128,512]{2,1,0:T(8,128)(2,1)S(1)} %get-tuple-element.67), channel_id=1, source_target_pairs={{0,24},{8,16},{16,8},{24,0},{1,25},{9,17},{17,9},{25,1},{2,26},{10... | collective-permute-start | bytes 786440 | tf_op jit(solution)/shard_map/ppermute | solution.py:21
  41.1 14.7 %collective-permute-start.18 = (bf16[8,32,512]{2,1,0:T(8,128)(2,1)S(1)}, bf16[8,32,512]{2,1,0:T(8,128)(2,1)S(1)}, u32[]{:S(2)}, u32[]{:S(2)}) collective-permute-start(bf16[8,32,512]{2,1,0:T(8,128)(2,1)S(1)} %shard_map.119.b), channel_id=1, source_target_pairs={{0,8},{8,0},{16,24},{24,16},{1,9},{9,1},{17,25},{25,17},{2,10},{10... | collective-permute-start | bytes 786440 | tf_op jit(solution)/shard_map/ppermute | solution.py:21
  41.6 14.1 %collective-permute-start.19 = (bf16[8,32,512]{2,1,0:T(8,128)(2,1)S(1)}, bf16[8,32,512]{2,1,0:T(8,128)(2,1)S(1)}, u32[]{:S(2)}, u32[]{:S(2)}) collective-permute-start(bf16[8,32,512]{2,1,0:T(8,128)(2,1)S(1)} %shard_map.115.a), channel_id=1, source_target_pairs={{0,16},{8,24},{16,0},{24,8},{1,17},{9,25},{17,1},{25,9},{2,18},{10... | collective-permute-start | bytes 786440 | tf_op jit(solution)/shard_map/ppermute | solution.py:21
  42.8 21.1 %collective-permute-start.17 = (bf16[8,32,512]{2,1,0:T(8,128)(2,1)S(1)}, bf16[8,32,512]{2,1,0:T(8,128)(2,1)S(1)}, u32[]{:S(2)}, u32[]{:S(2)}) collective-permute-start(bf16[8,32,512]{2,1,0:T(8,128)(2,1)S(1)} %collective-permute-done.16.b1), channel_id=1, source_target_pairs={{0,8},{8,0},{16,24},{24,16},{1,9},{9,1},{17,25},{25,17},{2,10},{10... | collective-permute-start | bytes 786440 | tf_op jit(solution)/shard_map/ppermute | solution.py:21
  44.4 19.4 %collective-permute-start.8 = (bf16[8,32,512]{2,1,0:T(8,128)(2,1)S(1)}, bf16[8,32,512]{2,1,0:T(8,128)(2,1)S(1)}, u32[]{:S(2)}, u32[]{:S(2)}) collective-permute-start(bf16[8,32,512]{2,1,0:T(8,128)(2,1)S(1)} %collective-permute-done.7.a0), channel_id=1, source_target_pairs={{0,16},{8,24},{16,0},{24,8},{1,17},{9,25},{17,1},{25,9},{2,18},{10... | collective-permute-start | bytes 786440 | tf_op jit(solution)/shard_map/ppermute | solution.py:21
  57.8 5.5 %collective-permute-start.23 = (f32[8,128]{1,0:T(8,128)S(1)}, f32[8,128]{1,0:T(8,128)S(1)}, u32[]{:S(2)}, u32[]{:S(2)}) collective-permute-start(f32[8,128]{1,0:T(8,128)S(1)} %get-tuple-element.72.rest_0_), channel_id=1, source_target_pairs={{0,24},{8,16},{16,8},{24,0},{1,25},{9,17},{17,9},{25,1},{2,26},{10... | collective-permute-start | bytes 12296 | tf_op jit(solution)/shard_map/ppermute | solution.py:21
  59.4 4.0 %collective-permute-start.22 = (f32[8,128]{1,0:T(8,128)S(1)}, f32[8,128]{1,0:T(8,128)S(1)}, u32[]{:S(2)}, u32[]{:S(2)}) collective-permute-start(f32[8,128]{1,0:T(8,128)S(1)} %get-tuple-element.72.rest_0_), channel_id=1, source_target_pairs={{0,16},{8,24},{16,0},{24,8},{1,17},{9,25},{17,1},{25,9},{2,18},{10... | collective-permute-start | bytes 12296 | tf_op jit(solution)/shard_map/ppermute | solution.py:21
  60.3 3.6 %collective-permute-start.21 = (f32[8,128]{1,0:T(8,128)S(1)}, f32[8,128]{1,0:T(8,128)S(1)}, u32[]{:S(2)}, u32[]{:S(2)}) collective-permute-start(f32[8,128]{1,0:T(8,128)S(1)} %get-tuple-element.72.rest_0_), channel_id=1, source_target_pairs={{0,8},{8,0},{16,24},{24,16},{1,9},{9,1},{17,25},{25,17},{2,10},{10... | collective-permute-start | bytes 12296 | tf_op jit(solution)/shard_map/ppermute | solution.py:21
